TPU v7x, 64 devices: a 2x2x8 block of a 4x4x8 slice. The times are simulated.
64 devices in a mesh: rep: 4 (over x, y), pool: 16 (over z, core).
Axes of the slice: x: 2, y: 2, z: 8, core: 2. Of those that a mesh axis runs over, the one named last changes fastest.
The devices are a block of a 4x4x8 slice.
Arguments:
- kv_pool: bfloat16 [2, 4096, 2, 16, 36, 64], P(None, ('rep', 'pool')), parts along dimension 1
- page_idx: int32 [16, 64, 4], P(None, ('rep', 'pool')), parts along dimension 1
- tok_hidden: bfloat16 [64, 64, 2304], P(('rep', 'pool')), parts along dimension 0
- attn_norm: bfloat16 [2, 2304], replicated
- w_query: bfloat16 [2, 2304, 2304], replicated
- w_key: bfloat16 [2, 2304, 2304], replicated
- w_value: bfloat16 [2, 2304, 2304], replicated
- w_out: bfloat16 [2, 2304, 2304], replicated
- mlp_norm: bfloat16 [2, 2304], replicated
- w_gate: bfloat16 [2, 2304, 5760], replicated
- w_up: bfloat16 [2, 2304, 5760], replicated
- w_down: bfloat16 [2, 5760, 2304], replicated
Outputs:
- output: bfloat16 [64, 64, 2304], P(('rep', 'pool')), parts along dimension 0
There are 4 independent parts. A program takes and returns all parts, laid end to end along the dimension named above; an argument that names none is the same for every part.
All inputs are finite; a program needn't handle non-finite values.
Results may differ from a plain program's by a relative error of at most 0.0166935.
Values are sent between devices in bfloat16 or wider.
A program may use at most 768 MiB of HBM per device.

v0:
```python
import functools
import jax
import jax.numpy as jnp
from jax import lax
from jax.experimental import pallas as pl
from jax.experimental.pallas import tpu as pltpu
from jax.sharding import PartitionSpec as P

NORM_EPS = 1e-6
ROPE_BASE = 10000.0
CHUNKS = 4
F32 = jnp.float32
BF16 = jnp.bfloat16


def rope_tables(offset, tokens, head_dim):
    positions = (offset + jnp.arange(tokens)).astype(F32)
    exponent = jnp.arange(head_dim // 2).astype(F32) * (-2.0 / head_dim)
    inv_freq = jnp.power(ROPE_BASE, exponent)
    angles = positions[:, None] * inv_freq[None, :]
    cosine, sine = jnp.cos(angles), jnp.sin(angles)
    return jnp.concatenate([cosine] * 4, axis=1), jnp.concatenate([-sine, sine] * 2, axis=1)


def rms_norm(vals, gain):
    vals_f = vals.astype(F32)
    inv_rms = lax.rsqrt(jnp.mean(vals_f * vals_f, axis=-1, keepdims=True) + NORM_EPS)
    return (vals_f * inv_rms * gain.astype(F32)).astype(BF16)


def pack_kernel(layer, idx_ref, kv_hbm, out_ref, pages, sems):
    depth, slots = pages.shape[0], pages.shape[1]
    page_len = pages.shape[4]
    pairs = out_ref.shape[2]
    req, reqs = pl.program_id(0), pl.num_programs(0)

    def read(r, j):
        slot = lax.rem(r, depth)
        return pltpu.make_async_copy(kv_hbm.at[layer, idx_ref[r, j]], pages.at[slot, j], sems.at[slot, j])

    @pl.when(req == 0)
    def _():
        for r in range(depth - 1):
            for j in range(slots):
                read(r, j).start()

    @pl.when(req + depth - 1 < reqs)
    def _():
        for j in range(slots):
            read(req + depth - 1, j).start()

    slot = lax.rem(req, depth)
    for j in range(slots):
        read(req, j).wait()
        rows = pl.ds(j * page_len, page_len)
        for part in range(2):
            for i in range(pairs):
                both = jnp.concatenate([pages[slot, j, part, 2 * i], pages[slot, j, part, 2 * i + 1]], axis=-1)
                out_ref[0, part, i, rows, :] = both


def pack_pages(kv_heads, idx, layer, depth=4):
    _, _, _, heads, page_len, dim = kv_heads.shape
    reqs, slots = idx.shape
    out_block = (1, 2, heads // 2, slots * page_len, 2 * dim)
    nbytes = kv_heads[0].size * 2
    return pl.pallas_call(
        functools.partial(pack_kernel, layer),
        grid=(reqs,),
        in_specs=[pl.BlockSpec(memory_space=pltpu.SMEM), pl.BlockSpec(memory_space=pl.ANY)],
        out_specs=pl.BlockSpec(out_block, lambda r: (r, 0, 0, 0, 0)),
        out_shape=jax.ShapeDtypeStruct((reqs,) + out_block[1:], BF16),
        scratch_shapes=[
            pltpu.VMEM((depth, slots, 2, heads, page_len, dim), BF16),
            pltpu.SemaphoreType.DMA((depth, slots)),
        ],
        compiler_params=pltpu.CompilerParams(dimension_semantics=('arbitrary',)),
        cost_estimate=pl.CostEstimate(flops=0, bytes_accessed=3 * nbytes, transcendentals=0),
        name='pack_pages',
    )(idx, kv_heads)


def qkv_kernel(layer, x_ref, gain_ref, cos_ref, sin_ref, wq_hbm, wk_hbm, wv_hbm, q_ref, k_ref, v_ref, normed, slab, sems):
    depth, tile = slab.shape[0], slab.shape[3]
    tiles = wq_hbm.shape[2] // tile
    weights = (wq_hbm, wk_hbm, wv_hbm)

    def read(t, i):
        slot = lax.rem(t, depth)
        cols = pl.ds(pl.multiple_of(t * tile, tile), tile)
        return pltpu.make_async_copy(weights[i].at[layer, :, cols], slab.at[slot, i], sems.at[slot, i])

    for t in range(depth):
        for i in range(3):
            read(t, i).start()

    normed[...] = rms_norm(x_ref[...], gain_ref[...])
    lane = lax.broadcasted_iota(jnp.int32, cos_ref.shape, 1)
    low = (lane % 64) < 32

    def one(t, _):
        slot = lax.rem(t, depth)
        for i, out_ref in enumerate((q_ref, k_ref, v_ref)):
            read(t, i).wait()
            proj = jnp.dot(normed[...], slab[slot, i], preferred_element_type=F32)
            for p in range(tile // 128):
                part = proj[:, p * 128:(p + 1) * 128]
                if i < 2:
                    swapped = jnp.where(low, pltpu.roll(part, 96, 1), pltpu.roll(part, 32, 1))
                    part = part * cos_ref[...] + swapped * sin_ref[...]
                out_ref[t * (tile // 128) + p] = part.astype(BF16)

        @pl.when(t + depth < tiles)
        def _():
            for i in range(3):
                read(t + depth, i).start()

        return 0

    lax.fori_loop(0, tiles, one, 0)


def qkv_proj(x, gain, cosine, sine, w_query, w_key, w_value, layer, tile=256, depth=4):
    tokens, width = x.shape
    cols = w_query.shape[2]
    vmem, hbm = pl.BlockSpec(memory_space=pltpu.VMEM), pl.BlockSpec(memory_space=pl.ANY)
    out = jax.ShapeDtypeStruct((cols // 128, tokens, 128), BF16)
    return pl.pallas_call(
        functools.partial(qkv_kernel, layer),
        in_specs=[vmem] * 4 + [hbm] * 3,
        out_specs=[vmem] * 3,
        out_shape=[out] * 3,
        scratch_shapes=[
            pltpu.VMEM((tokens, width), BF16),
            pltpu.VMEM((depth, 3, width, tile), BF16),
            pltpu.SemaphoreType.DMA((depth, 3)),
        ],
        cost_estimate=pl.CostEstimate(flops=6 * tokens * width * cols, bytes_accessed=6 * width * cols, transcendentals=0),
        name='qkv_proj',
    )(x, gain, cosine, sine, w_query, w_key, w_value)


def half_masks(shape, dtype):
    lane = lax.broadcasted_iota(jnp.int32, shape, 1)
    low = jnp.where(lane < 64, 1.0, 0.0)
    return low.astype(dtype), (1.0 - low).astype(dtype)


def block_diag(pair, low, high):
    return jnp.concatenate([pair * low, pair * high], axis=0)


def dot_t(a, b):
    return lax.dot_general(a, b, (((1,), (1,)), ((), ())), preferred_element_type=F32)


def layer_kernel(layer, group, scale, q_ref, k_ref, v_ref, x_ref, gain_ref, kv_hbm, wo_hbm, wg_hbm, wu_hbm, wd_hbm, out_ref,
                 kv, qbuf, obuf, loc, home, score, prob, rowwise, normed, total, wo, slab_in, slab_out,
                 kv_sem, q_send, q_recv, o_send, o_recv, wo_sem, sems):
    pairs, tokens, lanes = q_ref.shape
    half = pairs // 2
    rows = tokens // CHUNKS
    me = lax.axis_index('pool')
    right, left = lax.rem(me + 1, group), lax.rem(me + group - 1, group)
    toward = (right, left)

    barrier = pltpu.get_barrier_semaphore()
    for neighbour in toward:
        pl.semaphore_signal(barrier, inc=1, device_id={'pool': neighbour}, device_id_type=pl.DeviceIdType.MESH)
    pl.semaphore_wait(barrier, 2)

    def request_at(d, s):
        return lax.rem(me - s + group, group) if d == 0 else lax.rem(me + s, group)

    def kv_copy(d, s):
        return pltpu.make_async_copy(kv_hbm.at[request_at(d, s), :, pl.ds(half * d, half)], kv.at[d, s], kv_sem.at[d, s])

    def q_copy(d, s):
        return pltpu.make_async_remote_copy(
            src_ref=qbuf.at[d, s], dst_ref=qbuf.at[d, s + 1], send_sem=q_send.at[d, s], recv_sem=q_recv.at[d, s + 1],
            device_id={'pool': toward[d]}, device_id_type=pl.DeviceIdType.MESH)

    def q_first(d):
        return pltpu.make_async_remote_copy(
            src_ref=q_ref.at[pl.ds(half * d, half)], dst_ref=qbuf.at[d, 1], send_sem=q_send.at[d, 0], recv_sem=q_recv.at[d, 1],
            device_id={'pool': toward[d]}, device_id_type=pl.DeviceIdType.MESH)

    def o_copy(d, s, c):
        return pltpu.make_async_remote_copy(
            src_ref=obuf.at[d, s - 1, c], dst_ref=obuf.at[d, s, c], send_sem=o_send.at[d, s - 1, c], recv_sem=o_recv.at[d, s, c],
            device_id={'pool': toward[d]}, device_id_type=pl.DeviceIdType.MESH)

    for d in range(2):
        q_first(d).start()

    @pl.loop(0, group)
    def _(s):
        for d in range(2):
            kv_copy(d, s).start()

    depth, tile = slab_out.shape[0], slab_out.shape[1]
    tiles = wg_hbm.shape[2] // tile
    wo_tiles, wo_tile = wo.shape[0], wo.shape[2]

    def read_out(t):
        return pltpu.make_async_copy(wo_hbm.at[layer, :, pl.ds(t * wo_tile, wo_tile)], wo.at[t], wo_sem.at[t])

    def reads(t):
        slot = lax.rem(t, depth)
        cols = pl.ds(pl.multiple_of(t * tile, tile), tile)
        return (pltpu.make_async_copy(wg_hbm.at[layer, :, cols], slab_in.at[slot, 0], sems.at[slot, 0]),
                pltpu.make_async_copy(wu_hbm.at[layer, :, cols], slab_in.at[slot, 1], sems.at[slot, 1]),
                pltpu.make_async_copy(wd_hbm.at[layer, cols, :], slab_out.at[slot], sems.at[slot, 2]))

    for t in range(wo_tiles):
        read_out(t).start()
    for t in range(depth):
        for copy in reads(t):
            copy.start()

    low_b, high_b = half_masks((tokens, lanes), BF16)

    row_lane = lax.broadcasted_iota(jnp.int32, (rows, lanes), 1)
    row_low = row_lane < 64
    row_at = lax.broadcasted_iota(jnp.int32, (rows, lanes), 0)

    def local_part(d, dest, query_at, key_at, val_at, causal):
        for j in range(half):
            score[d, j] = dot_t(query_at(j), block_diag(key_at(j), low_b, high_b)) * scale
        for c in range(CHUNKS):
            here = slice(c * rows, (c + 1) * rows)
            tops = jnp.zeros((rows, lanes), F32)
            sums = jnp.ones((rows, lanes), F32)
            for j in range(half):
                part = score[d, j, here]
                if causal:
                    part = jnp.where(lax.rem(row_lane, 64) <= row_at + c * rows, part, -1e30)
                top0 = jnp.max(jnp.where(row_low, part, -jnp.inf), axis=1, keepdims=True)
                top1 = jnp.max(jnp.where(row_low, -jnp.inf, part), axis=1, keepdims=True)
                raised = jnp.exp(part - jnp.where(row_low, top0, top1))
                sum0 = jnp.sum(jnp.where(row_low, raised, 0.0), axis=1, keepdims=True)
                sum1 = jnp.sum(jnp.where(row_low, 0.0, raised), axis=1, keepdims=True)
                prob[d, j, here] = (raised * (1.0 / jnp.where(row_low, sum0, sum1))).astype(BF16)
                at0, at1 = row_lane == j, row_lane == 64 + j
                tops = jnp.where(at0, top0, jnp.where(at1, top1, tops))
                sums = jnp.where(at0, sum0, jnp.where(at1, sum1, sums))
            dest[d, c, half] = tops + jnp.log(sums)
        for j in range(half):
            out = jnp.dot(prob[d, j], block_diag(val_at(j), low_b, high_b), preferred_element_type=F32)
            for c in range(CHUNKS):
                dest[d, c, j] = out[c * rows:(c + 1) * rows]

    def weights(far, near):
        gap = far - near
        joint = jnp.maximum(far, near) + jnp.log(1.0 + jnp.exp(-jnp.abs(gap)))
        return 1.0 / (1.0 + jnp.exp(-gap)), joint

    def spread(stat, j):
        return jnp.where(row_low, stat[:, j:j + 1], stat[:, 64 + j:65 + j])

    def merge(d, c, far, near):
        weight, joint = weights(far[half], near[half])
        outs = [near[j] + spread(weight, j) * (far[j] - near[j]) for j in range(half)]
        return outs, joint

    for d in range(2):
        kv_copy(d, 0).wait()
        own = half * d
        local_part(d, home, lambda j: q_ref[own + j], lambda j: kv[d, 0, 0, j], lambda j: kv[d, 0, 1, j], False)
        local_part(d, loc, lambda j: q_ref[own + j], lambda j: k_ref[own + j], lambda j: v_ref[own + j], True)
        for c in range(CHUNKS):
            outs, joint = merge(d, c, home.at[d, c], loc.at[d, c])
            for j in range(half):
                home[d, c, j] = outs[j]
            home[d, c, half] = joint

    def step(s, _):
        for d in range(2):
            q_copy(d, s - 1).wait_recv()

            @pl.when(s < group - 1)
            def _():
                q_copy(d, s).start()

        for d in range(2):
            kv_copy(d, s).wait()
            local_part(d, loc, lambda j: qbuf[d, s, j], lambda j: kv[d, s, 0, j], lambda j: kv[d, s, 1, j], False)

        @pl.when(s == 1)
        def _():
            for d in range(2):
                for c in range(CHUNKS):
                    obuf[d, 1, c] = loc[d, c]

        for c in range(CHUNKS):
            for d in range(2):
                @pl.when(s > 1)
                def _():
                    o_copy(d, s, c).wait_recv()
                    outs, joint = merge(d, c, obuf.at[d, s, c], loc.at[d, c])
                    for j in range(half):
                        obuf[d, s, c, j] = outs[j]
                    obuf[d, s, c, half] = joint

                o_copy(d, s + 1, c).start()
        return 0

    lax.fori_loop(1, group, step, 0)

    for c in range(CHUNKS):
        for d in range(2):
            o_copy(d, group, c).wait_recv()
            outs, _ = merge(d, c, obuf.at[d, group, c], home.at[d, c])
            for j in range(half):
                at = (half * d + j) * lanes
                rowwise[c * rows:(c + 1) * rows, at:at + lanes] = outs[j].astype(BF16)

    for t in range(wo_tiles):
        read_out(t).wait()
        cols = slice(t * wo_tile, (t + 1) * wo_tile)
        proj = jnp.dot(rowwise[...], wo[t], preferred_element_type=F32)
        out_ref[:, cols] = (x_ref[:, cols].astype(F32) + proj).astype(BF16)
    normed[...] = rms_norm(out_ref[...], gain_ref[...])
    total[...] = jnp.zeros_like(total)

    def one(t, _):
        slot = lax.rem(t, depth)
        gate_read, up_read, down_read = reads(t)
        gate_read.wait()
        gate = jnp.dot(normed[...], slab_in[slot, 0], preferred_element_type=F32)
        up_read.wait()
        upper = jnp.dot(normed[...], slab_in[slot, 1], preferred_element_type=F32)
        inner = (jax.nn.silu(gate) * upper).astype(BF16)
        down_read.wait()
        total[...] += jnp.dot(inner, slab_out[slot], preferred_element_type=F32)

        @pl.when(t + depth < tiles)
        def _():
            for copy in reads(t + depth):
                copy.start()

        return 0

    lax.fori_loop(0, tiles, one, 0)
    out_ref[...] = (out_ref[...].astype(F32) + total[...]).astype(BF16)

    for d in range(2):
        q_first(d).wait_send()

    @pl.loop(1, group)
    def _(s):
        for d in range(2):
            @pl.when(s < group - 1)
            def _():
                q_copy(d, s).wait_send()

            for c in range(CHUNKS):
                o_copy(d, s + 1, c).wait_send()


def layer_rest(x, query, key, val, packed, gain, w_out, w_gate, w_up, w_down, layer, group, scale, tile=384, depth=4, wo_tile=768):
    pairs, tokens, lanes = query.shape
    width, attn, inner = x.shape[1], w_out.shape[1], w_gate.shape[2]
    half = pairs // 2
    rows = tokens // CHUNKS
    sem = pltpu.SemaphoreType.DMA
    vmem, hbm = pl.BlockSpec(memory_space=pltpu.VMEM), pl.BlockSpec(memory_space=pl.ANY)
    scratch = [
        pltpu.VMEM((2, group, 2, half, tokens, lanes), BF16),
        pltpu.VMEM((2, group, half, tokens, lanes), BF16),
        pltpu.VMEM((2, group + 1, CHUNKS, half + 1, rows, lanes), F32),
        pltpu.VMEM((2, CHUNKS, half + 1, rows, lanes), F32),
        pltpu.VMEM((2, CHUNKS, half + 1, rows, lanes), F32),
        pltpu.VMEM((2, half, tokens, lanes), F32),
        pltpu.VMEM((2, half, tokens, lanes), BF16),
        pltpu.VMEM((tokens, attn), BF16),
        pltpu.VMEM((tokens, width), BF16),
        pltpu.VMEM((tokens, width), F32),
        pltpu.VMEM((width // wo_tile, attn, wo_tile), BF16),
        pltpu.VMEM((depth, 2, width, tile), BF16),
        pltpu.VMEM((depth, tile, width), BF16),
        sem((2, group)),
        sem((2, group)),
        sem((2, group)),
        sem((2, group + 1, CHUNKS)),
        sem((2, group + 1, CHUNKS)),
        sem((width // wo_tile,)),
        sem((depth, 3)),
    ]
    return pl.pallas_call(
        functools.partial(layer_kernel, layer, group, scale),
        out_shape=jax.ShapeDtypeStruct(x.shape, BF16),
        in_specs=[vmem] * 5 + [hbm] * 5,
        out_specs=vmem,
        scratch_shapes=scratch,
        compiler_params=pltpu.CompilerParams(collective_id=layer, has_side_effects=True, vmem_limit_bytes=67_000_000),
        name='layer_rest',
    )(query, key, val, x, gain, packed, w_out, w_gate, w_up, w_down)


def solution(mesh):
    group = mesh.shape['pool']

    def local_program(kv_local, idx_local, hid_local, attn_norm, w_query, w_key, w_value, w_out, mlp_norm, w_gate, w_up, w_down):
        layers, _, _, page_len, _, dim = kv_local.shape
        prefix = group * idx_local.shape[2] * page_len
        cosine, sine = rope_tables(prefix, hid_local.shape[1], dim)
        idx = idx_local[:, 0, :]
        kv_heads = jnp.transpose(kv_local, (0, 1, 2, 4, 3, 5))
        x = hid_local[0]
        for layer in range(layers):
            packed = pack_pages(kv_heads, idx, layer)
            query, key, val = qkv_proj(x, attn_norm[layer:layer + 1], cosine, sine, w_query, w_key, w_value, layer)
            x = layer_rest(x, query, key, val, packed, mlp_norm[layer:layer + 1], w_out, w_gate, w_up, w_down, layer, group, dim ** -0.5)
        return x[None]

    data_specs = (P(None, ('rep', 'pool')), P(None, ('rep', 'pool'), None), P(('rep', 'pool')))
    return jax.shard_map(local_program, mesh=mesh, in_specs=data_specs + (P(),) * 9, out_specs=P(('rep', 'pool')), check_vma=False)
```

profile of v0, /device:TPU:21, one launch (start us, length us, event | category | flops | bytes accessed | tf_op | source)
XLA Modules:
  0.0 292.9 jit_solution(4420263503636903012)
XLA Ops:
  0.0 0.2 fusion
  0.2 0.7 pad_maximum_fusion
  1.0 1.4 fusion.2
  2.4 0.0 copy-start.1
  2.4 16.0 %qkv_proj.2 = (bf16[18,64,128]{2,1,0:T(8,128)(2,1)}, bf16[18,64,128]{2,1,0:T(8,128)(2,1)}, bf16[18,64,128]{2,1,0:T(8,128)(2,1)}) custom-call(bf16[64,2304]{1,0:T(8,128)(2,1)} %bitcast.6, bf16[1,2304]{1,0:T(2,128)(2,1)} %get-tuple-element.20.gain_ref, f32[64,128]{1,0:T(8,128)} %get-tuple-element.24.cos_ref, f32[64,128]{1,0:T(8,128)} %get-tuple-element.25.sin_ref, ...), custom_call_target="tpu_custom_call" | custom-call | flops 2038431744 | bytes 31850496 | tf_op jit(solution)/shard_map/qkv_proj/pallas_call | solution.py:128
  18.3 0.0 copy-done.1
  18.4 0.7 copy.13.idx_ref
  19.0 0.0 copy-start
  19.0 13.0 %pack_pages.2.kv_hbm = bf16[16,2,18,64,128]{4,3,2,1,0:T(8,128)(2,1)} custom-call(s32[16,4]{1,0:T(8,128)} %copy.13.idx_ref, bf16[2,64,2,36,16,64]{5,4,3,2,1,0:T(8,128)(2,1)} %bitcast.4), custom_call_target="tpu_custom_call" | custom-call | bytes 28311552 | tf_op jit(solution)/shard_map/pack_pages/pallas_call | solution.py:67
  32.0 0.0 copy-done
  32.0 0.6 fusion.1
  32.6 116.2 %layer_rest.2.x_ref = bf16[64,2304]{1,0:T(8,128)(2,1)} custom-call(bf16[18,64,128]{2,1,0:T(8,128)(2,1)} %get-tuple-element.11.q_ref, bf16[18,64,128]{2,1,0:T(8,128)(2,1)} %get-tuple-element.12.k_ref, bf16[18,64,128]{2,1,0:T(8,128)(2,1)} %get-tuple-element.13.v_ref, bf16[64,2304]{1,0:T(8,128)(2,1)} %bitcast.7, bf16[1,2304]{1,0:T(2,128)(2,1)} %get-tuple-element.18.gain_ref, ...), custom_call_target="tpu_custom_call" | custom-call | tf_op jit(solution)/shard_map/layer_rest/pallas_call | solution.py:390
  148.8 16.0 %qkv_proj.3 = (bf16[18,64,128]{2,1,0:T(8,128)(2,1)}, bf16[18,64,128]{2,1,0:T(8,128)(2,1)}, bf16[18,64,128]{2,1,0:T(8,128)(2,1)}) custom-call(bf16[64,2304]{1,0:T(8,128)(2,1)} %layer_rest.2.x_ref, bf16[1,2304]{1,0:T(2,128)(2,1)} %get-tuple-element.19.gain_ref, f32[64,128]{1,0:T(8,128)} %get-tuple-element.24.cos_ref, f32[64,128]{1,0:T(8,128)} %get-tuple-element.25.sin_ref, ...), custom_call_target="tpu_custom_call" | custom-call | flops 2038431744 | bytes 31850496 | tf_op jit(solution)/shard_map/qkv_proj/pallas_call | solution.py:128
  164.8 12.9 %pack_pages.3.kv_hbm = bf16[16,2,18,64,128]{4,3,2,1,0:T(8,128)(2,1)} custom-call(s32[16,4]{1,0:T(8,128)} %copy.13.idx_ref, bf16[2,64,2,36,16,64]{5,4,3,2,1,0:T(8,128)(2,1)} %bitcast.5), custom_call_target="tpu_custom_call" | custom-call | bytes 28311552 | tf_op jit(solution)/shard_map/pack_pages/pallas_call | solution.py:67
  177.7 113.5 %layer_rest.3 = bf16[64,2304]{1,0:T(8,128)(2,1)} custom-call(bf16[18,64,128]{2,1,0:T(8,128)(2,1)} %get-tuple-element.14.q_ref, bf16[18,64,128]{2,1,0:T(8,128)(2,1)} %get-tuple-element.15.k_ref, bf16[18,64,128]{2,1,0:T(8,128)(2,1)} %get-tuple-element.16.v_ref, bf16[64,2304]{1,0:T(8,128)(2,1)} %layer_rest.2.x_ref, bf16[1,2304]{1,0:T(2,128)(2,1)} %get-tuple-element.17.gain_ref, ...), custom_call_target="tpu_custom_call" | custom-call | tf_op jit(solution)/shard_map/layer_rest/pallas_call | solution.py:390
  291.2 1.7 copy.16
  (2 shorter events, 0.0 us)
Async XLA Ops:
  2.4 16.0 %copy-start.1 = (s32[16,1,4]{0,2,1:T(4,128)S(1)}, s32[16,1,4]{0,2,1:T(4,128)}, u32[]{:S(2)}) copy-start(s32[16,1,4]{0,2,1:T(4,128)} %param.13) | copy-start | bytes 772
  19.0 13.0 %copy-start = (bf16[2,2304]{1,0:T(2,128)(2,1)S(1)}, bf16[2,2304]{1,0:T(2,128)(2,1)}, u32[]{:S(2)}) copy-start(bf16[2,2304]{1,0:T(2,128)(2,1)} %param.20) | copy-start | bytes 27652
where the time goes:
time: 295 us; the launch traced here: 293 us
  Pallas kernels  288 us (98%)
  local copies, waits for them, and re-layouts  4.39 us (1%)
    pallas_call x2, Pallas kernels, layer_rest(): pl.pallas_call(functools.partial(layer_kernel, layer, group, scale), out_...  230 us
    pallas_call x2, Pallas kernels, qkv_proj(): pl.pallas_call(functools.partial(qkv_kernel, layer), in_specs=[vmem] * 4...  31.9 us
    pallas_call x2, Pallas kernels, pack_pages(): pl.pallas_call(functools.partial(pack_kernel, layer), grid=(reqs,), in_sp...  25.8 us

commit v1 on v0

--- a/solution.py
+++ b/solution.py
@@ -28,77 +28,39 @@
     return (vals_f * inv_rms * gain.astype(F32)).astype(BF16)
 
 
-def pack_kernel(layer, idx_ref, kv_hbm, out_ref, pages, sems):
-    depth, slots = pages.shape[0], pages.shape[1]
-    page_len = pages.shape[4]
-    pairs = out_ref.shape[2]
-    req, reqs = pl.program_id(0), pl.num_programs(0)
-
-    def read(r, j):
-        slot = lax.rem(r, depth)
-        return pltpu.make_async_copy(kv_hbm.at[layer, idx_ref[r, j]], pages.at[slot, j], sems.at[slot, j])
-
-    @pl.when(req == 0)
-    def _():
-        for r in range(depth - 1):
-            for j in range(slots):
-                read(r, j).start()
-
-    @pl.when(req + depth - 1 < reqs)
-    def _():
-        for j in range(slots):
-            read(req + depth - 1, j).start()
-
-    slot = lax.rem(req, depth)
-    for j in range(slots):
-        read(req, j).wait()
-        rows = pl.ds(j * page_len, page_len)
-        for part in range(2):
-            for i in range(pairs):
-                both = jnp.concatenate([pages[slot, j, part, 2 * i], pages[slot, j, part, 2 * i + 1]], axis=-1)
-                out_ref[0, part, i, rows, :] = both
-
-
-def pack_pages(kv_heads, idx, layer, depth=4):
-    _, _, _, heads, page_len, dim = kv_heads.shape
-    reqs, slots = idx.shape
-    out_block = (1, 2, heads // 2, slots * page_len, 2 * dim)
-    nbytes = kv_heads[0].size * 2
-    return pl.pallas_call(
-        functools.partial(pack_kernel, layer),
-        grid=(reqs,),
-        in_specs=[pl.BlockSpec(memory_space=pltpu.SMEM), pl.BlockSpec(memory_space=pl.ANY)],
-        out_specs=pl.BlockSpec(out_block, lambda r: (r, 0, 0, 0, 0)),
-        out_shape=jax.ShapeDtypeStruct((reqs,) + out_block[1:], BF16),
-        scratch_shapes=[
-            pltpu.VMEM((depth, slots, 2, heads, page_len, dim), BF16),
-            pltpu.SemaphoreType.DMA((depth, slots)),
-        ],
-        compiler_params=pltpu.CompilerParams(dimension_semantics=('arbitrary',)),
-        cost_estimate=pl.CostEstimate(flops=0, bytes_accessed=3 * nbytes, transcendentals=0),
-        name='pack_pages',
-    )(idx, kv_heads)
-
-
-def qkv_kernel(layer, x_ref, gain_ref, cos_ref, sin_ref, wq_hbm, wk_hbm, wv_hbm, q_ref, k_ref, v_ref, normed, slab, sems):
+def front_kernel(layer, idx_ref, x_ref, gain_ref, cos_ref, sin_ref, wq_hbm, wk_hbm, wv_hbm, kv_hbm,
+                 q_ref, k_ref, v_ref, packed_hbm, normed, slab, pages, block, sems, page_sems, out_sems):
     depth, tile = slab.shape[0], slab.shape[3]
     tiles = wq_hbm.shape[2] // tile
     weights = (wq_hbm, wk_hbm, wv_hbm)
+    ahead, slots, page_len = pages.shape[0], pages.shape[1], pages.shape[4]
+    reqs, pairs = idx_ref.shape[0], block.shape[2]
 
     def read(t, i):
         slot = lax.rem(t, depth)
         cols = pl.ds(pl.multiple_of(t * tile, tile), tile)
         return pltpu.make_async_copy(weights[i].at[layer, :, cols], slab.at[slot, i], sems.at[slot, i])
 
+    def read_page(r, j):
+        slot = lax.rem(r, ahead)
+        return pltpu.make_async_copy(kv_hbm.at[layer, idx_ref[r, j]], pages.at[slot, j], page_sems.at[slot, j])
+
+    def write(r):
+        slot = lax.rem(r, 2)
+        return pltpu.make_async_copy(block.at[slot], packed_hbm.at[r], out_sems.at[slot])
+
     for t in range(depth):
         for i in range(3):
             read(t, i).start()
+    for r in range(ahead):
+        for j in range(slots):
+            read_page(r, j).start()
 
     normed[...] = rms_norm(x_ref[...], gain_ref[...])
     lane = lax.broadcasted_iota(jnp.int32, cos_ref.shape, 1)
     low = (lane % 64) < 32
 
-    def one(t, _):
+    def project(t, _):
         slot = lax.rem(t, depth)
         for i, out_ref in enumerate((q_ref, k_ref, v_ref)):
             read(t, i).wait()
@@ -110,34 +72,66 @@
                     part = part * cos_ref[...] + swapped * sin_ref[...]
                 out_ref[t * (tile // 128) + p] = part.astype(BF16)
 
-        @pl.when(t + depth < tiles)
+            @pl.when(t + depth < tiles)
+            def _():
+                read(t + depth, i).start()
+
+        return 0
+
+    lax.fori_loop(0, tiles, project, 0)
+
+    def pack(r, _):
+        slot, out_slot = lax.rem(r, ahead), lax.rem(r, 2)
+
+        @pl.when(r >= 2)
         def _():
-            for i in range(3):
-                read(t + depth, i).start()
+            write(r - 2).wait()
+
+        for j in range(slots):
+            read_page(r, j).wait()
+            rows = pl.ds(j * page_len, page_len)
+            for part in range(2):
+                for i in range(pairs):
+                    both = jnp.concatenate([pages[slot, j, part, 2 * i], pages[slot, j, part, 2 * i + 1]], axis=-1)
+                    block[out_slot, part, i, rows, :] = both
+        write(r).start()
+
+        @pl.when(r + ahead < reqs)
+        def _():
+            for j in range(slots):
+                read_page(r + ahead, j).start()
 
         return 0
 
-    lax.fori_loop(0, tiles, one, 0)
-
-
-def qkv_proj(x, gain, cosine, sine, w_query, w_key, w_value, layer, tile=256, depth=4):
+    lax.fori_loop(0, reqs, pack, 0)
+    for r in (reqs - 2, reqs - 1):
+        write(r).wait()
+
+
+def layer_front(x, idx, gain, cosine, sine, w_query, w_key, w_value, kv_heads, layer, tile=256, depth=4, ahead=8):
     tokens, width = x.shape
     cols = w_query.shape[2]
+    _, _, _, heads, page_len, dim = kv_heads.shape
+    reqs, slots = idx.shape
+    block = (2, heads // 2, slots * page_len, 2 * dim)
     vmem, hbm = pl.BlockSpec(memory_space=pltpu.VMEM), pl.BlockSpec(memory_space=pl.ANY)
     out = jax.ShapeDtypeStruct((cols // 128, tokens, 128), BF16)
     return pl.pallas_call(
-        functools.partial(qkv_kernel, layer),
-        in_specs=[vmem] * 4 + [hbm] * 3,
-        out_specs=[vmem] * 3,
-        out_shape=[out] * 3,
+        functools.partial(front_kernel, layer),
+        in_specs=[pl.BlockSpec(memory_space=pltpu.SMEM)] + [vmem] * 4 + [hbm] * 4,
+        out_specs=[vmem] * 3 + [hbm],
+        out_shape=[out] * 3 + [jax.ShapeDtypeStruct((reqs,) + block, BF16)],
         scratch_shapes=[
             pltpu.VMEM((tokens, width), BF16),
             pltpu.VMEM((depth, 3, width, tile), BF16),
+            pltpu.VMEM((ahead, slots, 2, heads, page_len, dim), BF16),
+            pltpu.VMEM((2,) + block, BF16),
             pltpu.SemaphoreType.DMA((depth, 3)),
+            pltpu.SemaphoreType.DMA((ahead, slots)),
+            pltpu.SemaphoreType.DMA((2,)),
         ],
-        cost_estimate=pl.CostEstimate(flops=6 * tokens * width * cols, bytes_accessed=6 * width * cols, transcendentals=0),
-        name='qkv_proj',
-    )(x, gain, cosine, sine, w_query, w_key, w_value)
+        name='layer_front',
+    )(idx, x, gain, cosine, sine, w_query, w_key, w_value, kv_heads)
 
 
 def half_masks(shape, dtype):
@@ -155,8 +149,8 @@
 
 
 def layer_kernel(layer, group, scale, q_ref, k_ref, v_ref, x_ref, gain_ref, kv_hbm, wo_hbm, wg_hbm, wu_hbm, wd_hbm, out_ref,
-                 kv, qbuf, obuf, loc, home, score, prob, rowwise, normed, total, wo, slab_in, slab_out,
-                 kv_sem, q_send, q_recv, o_send, o_recv, wo_sem, sems):
+                 kv, qbuf, obuf, loc, home, score, prob, rowwise, mid, peer_mid, normed, total, peer_total, wo, slab_in, slab_out,
+                 kv_sem, q_send, q_recv, o_send, o_recv, wo_sem, sems, peer_send, peer_recv):
     pairs, tokens, lanes = q_ref.shape
     half = pairs // 2
     rows = tokens // CHUNKS
@@ -187,7 +181,7 @@
 
     def o_copy(d, s, c):
         return pltpu.make_async_remote_copy(
-            src_ref=obuf.at[d, s - 1, c], dst_ref=obuf.at[d, s, c], send_sem=o_send.at[d, s - 1, c], recv_sem=o_recv.at[d, s, c],
+            src_ref=obuf.at[d, s - 2, c], dst_ref=obuf.at[d, s - 1, c], send_sem=o_send.at[d, s - 2, c], recv_sem=o_recv.at[d, s - 1, c],
             device_id={'pool': toward[d]}, device_id_type=pl.DeviceIdType.MESH)
 
     for d in range(2):
@@ -205,8 +199,19 @@
     def read_out(t):
         return pltpu.make_async_copy(wo_hbm.at[layer, :, pl.ds(t * wo_tile, wo_tile)], wo.at[t], wo_sem.at[t])
 
-    def reads(t):
-        slot = lax.rem(t, depth)
+    core = lax.rem(me, 2)
+    peer = me + 1 - 2 * core
+    most = (tiles + 1) // 2
+    first, count = core * most, most - core * (2 * most - tiles)
+
+    def to_peer(i, src, dst):
+        return pltpu.make_async_remote_copy(
+            src_ref=src, dst_ref=dst, send_sem=peer_send.at[i], recv_sem=peer_recv.at[i],
+            device_id={'pool': peer}, device_id_type=pl.DeviceIdType.MESH)
+
+    def reads(n):
+        slot = lax.rem(n, depth)
+        t = first + n
         cols = pl.ds(pl.multiple_of(t * tile, tile), tile)
         return (pltpu.make_async_copy(wg_hbm.at[layer, :, cols], slab_in.at[slot, 0], sems.at[slot, 0]),
                 pltpu.make_async_copy(wu_hbm.at[layer, :, cols], slab_in.at[slot, 1], sems.at[slot, 1]),
@@ -290,17 +295,17 @@
         def _():
             for d in range(2):
                 for c in range(CHUNKS):
-                    obuf[d, 1, c] = loc[d, c]
+                    obuf[d, 0, c] = loc[d, c]
 
         for c in range(CHUNKS):
             for d in range(2):
                 @pl.when(s > 1)
                 def _():
                     o_copy(d, s, c).wait_recv()
-                    outs, joint = merge(d, c, obuf.at[d, s, c], loc.at[d, c])
+                    outs, joint = merge(d, c, obuf.at[d, s - 1, c], loc.at[d, c])
                     for j in range(half):
-                        obuf[d, s, c, j] = outs[j]
-                    obuf[d, s, c, half] = joint
+                        obuf[d, s - 1, c, j] = outs[j]
+                    obuf[d, s - 1, c, half] = joint
 
                 o_copy(d, s + 1, c).start()
         return 0
@@ -310,7 +315,7 @@
     for c in range(CHUNKS):
         for d in range(2):
             o_copy(d, group, c).wait_recv()
-            outs, _ = merge(d, c, obuf.at[d, group, c], home.at[d, c])
+            outs, _ = merge(d, c, obuf.at[d, group - 1, c], home.at[d, c])
             for j in range(half):
                 at = (half * d + j) * lanes
                 rowwise[c * rows:(c + 1) * rows, at:at + lanes] = outs[j].astype(BF16)
@@ -319,13 +324,17 @@
         read_out(t).wait()
         cols = slice(t * wo_tile, (t + 1) * wo_tile)
         proj = jnp.dot(rowwise[...], wo[t], preferred_element_type=F32)
-        out_ref[:, cols] = (x_ref[:, cols].astype(F32) + proj).astype(BF16)
-    normed[...] = rms_norm(out_ref[...], gain_ref[...])
+        mid[:, cols] = (x_ref[:, cols].astype(F32) + proj).astype(BF16)
+    share = to_peer(0, mid, peer_mid)
+    share.start()
+    normed[:tokens] = rms_norm(mid[...], gain_ref[...])
     total[...] = jnp.zeros_like(total)
-
-    def one(t, _):
-        slot = lax.rem(t, depth)
-        gate_read, up_read, down_read = reads(t)
+    share.wait_recv()
+    normed[tokens:] = rms_norm(peer_mid[...], gain_ref[...])
+
+    def one(n, _):
+        slot = lax.rem(n, depth)
+        gate_read, up_read, down_read = reads(n)
         gate_read.wait()
         gate = jnp.dot(normed[...], slab_in[slot, 0], preferred_element_type=F32)
         up_read.wait()
@@ -334,15 +343,20 @@
         down_read.wait()
         total[...] += jnp.dot(inner, slab_out[slot], preferred_element_type=F32)
 
-        @pl.when(t + depth < tiles)
+        @pl.when(n + depth < count)
         def _():
-            for copy in reads(t + depth):
+            for copy in reads(n + depth):
                 copy.start()
 
         return 0
 
-    lax.fori_loop(0, tiles, one, 0)
-    out_ref[...] = (out_ref[...].astype(F32) + total[...]).astype(BF16)
+    lax.fori_loop(0, count, one, 0)
+    back = to_peer(1, total.at[pl.ds(tokens, tokens)], peer_total)
+    back.start()
+    back.wait_recv()
+    out_ref[...] = (mid[...].astype(F32) + (total[:tokens] + peer_total[...])).astype(BF16)
+    share.wait_send()
+    back.wait_send()
 
     for d in range(2):
         q_first(d).wait_send()
@@ -368,13 +382,16 @@
     scratch = [
         pltpu.VMEM((2, group, 2, half, tokens, lanes), BF16),
         pltpu.VMEM((2, group, half, tokens, lanes), BF16),
-        pltpu.VMEM((2, group + 1, CHUNKS, half + 1, rows, lanes), F32),
+        pltpu.VMEM((2, group, CHUNKS, half + 1, rows, lanes), F32),
         pltpu.VMEM((2, CHUNKS, half + 1, rows, lanes), F32),
         pltpu.VMEM((2, CHUNKS, half + 1, rows, lanes), F32),
         pltpu.VMEM((2, half, tokens, lanes), F32),
         pltpu.VMEM((2, half, tokens, lanes), BF16),
         pltpu.VMEM((tokens, attn), BF16),
         pltpu.VMEM((tokens, width), BF16),
+        pltpu.VMEM((tokens, width), BF16),
+        pltpu.VMEM((2 * tokens, width), BF16),
+        pltpu.VMEM((2 * tokens, width), F32),
         pltpu.VMEM((tokens, width), F32),
         pltpu.VMEM((width // wo_tile, attn, wo_tile), BF16),
         pltpu.VMEM((depth, 2, width, tile), BF16),
@@ -382,10 +399,12 @@
         sem((2, group)),
         sem((2, group)),
         sem((2, group)),
-        sem((2, group + 1, CHUNKS)),
-        sem((2, group + 1, CHUNKS)),
+        sem((2, group, CHUNKS)),
+        sem((2, group, CHUNKS)),
         sem((width // wo_tile,)),
         sem((depth, 3)),
+        sem((2,)),
+        sem((2,)),
     ]
     return pl.pallas_call(
         functools.partial(layer_kernel, layer, group, scale),
@@ -409,8 +428,8 @@
         kv_heads = jnp.transpose(kv_local, (0, 1, 2, 4, 3, 5))
         x = hid_local[0]
         for layer in range(layers):
-            packed = pack_pages(kv_heads, idx, layer)
-            query, key, val = qkv_proj(x, attn_norm[layer:layer + 1], cosine, sine, w_query, w_key, w_value, layer)
+            query, key, val, packed = layer_front(
+                x, idx, attn_norm[layer:layer + 1], cosine, sine, w_query, w_key, w_value, kv_heads, layer)
             x = layer_rest(x, query, key, val, packed, mlp_norm[layer:layer + 1], w_out, w_gate, w_up, w_down, layer, group, dim ** -0.5)
         return x[None]
 

time: 295 us -> 284 us (0.963)
  Pallas kernels: 288 us -> 277 us
    pallas_call x2, Pallas kernels: 230 us -> 219 us  [layer_rest(): pl.pallas_call(functools.partial(layer_kernel, layer, group, scale), out_...]
    pallas_call x4 -> x2, Pallas kernels: 57.8 us -> 57.5 us  [layer_front(): pl.pallas_call(functools.partial(front_kernel, layer), in_specs=[pl.Block...]
where the time goes in v1:
time: 284 us
  Pallas kernels  277 us (98%)
  local copies, waits for them, and re-layouts  5.83 us (2%)
    pallas_call x2, Pallas kernels, layer_rest(): pl.pallas_call(functools.partial(layer_kernel, layer, group, scale), out_...  219 us
    pallas_call x2, Pallas kernels, layer_front(): pl.pallas_call(functools.partial(front_kernel, layer), in_specs=[pl.Block...  57.5 us

profile of v1, /device:TPU:21, one launch (start us, length us, event | category | flops | bytes accessed | tf_op | source)
XLA Modules:
  0.0 283.7 jit_solution(1161203929282976409)
XLA Ops:
  0.0 1.4 copy.14.idx_ref
  1.4 1.4 fusion.2
  2.8 1.4 fusion.1
  4.1 0.2 fusion
  4.3 0.7 pad_maximum_fusion
  5.1 28.7 %layer_front.2 = (bf16[18,64,128]{2,1,0:T(8,128)(2,1)}, bf16[18,64,128]{2,1,0:T(8,128)(2,1)}, bf16[18,64,128]{2,1,0:T(8,128)(2,1)}, bf16[16,2,18,64,128]{4,3,2,1,0:T(8,128)(2,1)}) custom-call(s32[16,4]{1,0:T(8,128)} %copy.14.idx_ref, bf16[64,2304]{1,0:T(8,128)(2,1)} %bitcast.6, bf16[1,2304]{1,0:T(2,128)(2,1)} %get-tuple-element.24.gain_ref, ...), custom_call_target="tpu_custom_call" | custom-call | tf_op jit(solution)/shard_map/layer_front/pallas_call | solution.py:119
  33.8 112.2 %layer_rest.2.x_ref = bf16[64,2304]{1,0:T(8,128)(2,1)} custom-call(bf16[18,64,128]{2,1,0:T(8,128)(2,1)} %get-tuple-element.13.q_ref, bf16[18,64,128]{2,1,0:T(8,128)(2,1)} %get-tuple-element.14.k_ref, bf16[18,64,128]{2,1,0:T(8,128)(2,1)} %get-tuple-element.15.v_ref, bf16[64,2304]{1,0:T(8,128)(2,1)} %bitcast.7, bf16[1,2304]{1,0:T(2,128)(2,1)} %get-tuple-element.22.gain_ref, ...), custom_call_target="tpu_custom_call" | custom-call | tf_op jit(solution)/shard_map/layer_rest/pallas_call | solution.py:409
  146.1 28.8 %layer_front.3 = (bf16[18,64,128]{2,1,0:T(8,128)(2,1)}, bf16[18,64,128]{2,1,0:T(8,128)(2,1)}, bf16[18,64,128]{2,1,0:T(8,128)(2,1)}, bf16[16,2,18,64,128]{4,3,2,1,0:T(8,128)(2,1)}) custom-call(s32[16,4]{1,0:T(8,128)} %copy.14.idx_ref, bf16[64,2304]{1,0:T(8,128)(2,1)} %layer_rest.2.x_ref, bf16[1,2304]{1,0:T(2,128)(2,1)} %get-tuple-element.23.gain_ref, ...), custom_call_target="tpu_custom_call" | custom-call | tf_op jit(solution)/shard_map/layer_front/pallas_call | solution.py:119
  174.9 107.1 %layer_rest.3 = bf16[64,2304]{1,0:T(8,128)(2,1)} custom-call(bf16[18,64,128]{2,1,0:T(8,128)(2,1)} %get-tuple-element.17.q_ref, bf16[18,64,128]{2,1,0:T(8,128)(2,1)} %get-tuple-element.18.k_ref, bf16[18,64,128]{2,1,0:T(8,128)(2,1)} %get-tuple-element.19.v_ref, bf16[64,2304]{1,0:T(8,128)(2,1)} %layer_rest.2.x_ref, bf16[1,2304]{1,0:T(2,128)(2,1)} %get-tuple-element.21.gain_ref, ...), custom_call_target="tpu_custom_call" | custom-call | tf_op jit(solution)/shard_map/layer_rest/pallas_call | solution.py:409
  282.0 1.7 copy.16
  (2 shorter events, 0.0 us)

commit v2 on v1

--- a/solution.py
+++ b/solution.py
@@ -56,9 +56,33 @@
         for j in range(slots):
             read_page(r, j).start()
 
-    normed[...] = rms_norm(x_ref[...], gain_ref[...])
+    normed[...] = rms_norm(x_ref[...], gain_ref[layer:layer + 1])
     lane = lax.broadcasted_iota(jnp.int32, cos_ref.shape, 1)
     low = (lane % 64) < 32
+
+    def pack(r):
+        slot, out_slot = lax.rem(r, ahead), lax.rem(r, 2)
+
+        @pl.when(r >= 2)
+        def _():
+            write(r - 2).wait()
+
+        for j in range(slots):
+            read_page(r, j).wait()
+        for j in range(slots):
+            rows = pl.ds(j * page_len, page_len)
+            for part in range(2):
+                for i in range(pairs):
+                    both = jnp.concatenate([pages[slot, j, part, 2 * i], pages[slot, j, part, 2 * i + 1]], axis=-1)
+                    block[out_slot, part, i, rows, :] = both
+        write(r).start()
+
+        @pl.when(r + ahead < reqs)
+        def _():
+            for j in range(slots):
+                read_page(r + ahead, j).start()
+
+    per = -(-reqs // tiles)
 
     def project(t, _):
         slot = lax.rem(t, depth)
@@ -76,34 +100,16 @@
             def _():
                 read(t + depth, i).start()
 
+        for n in range(per):
+            r = t * per + n
+
+            @pl.when(r < reqs)
+            def _():
+                pack(r)
+
         return 0
 
     lax.fori_loop(0, tiles, project, 0)
-
-    def pack(r, _):
-        slot, out_slot = lax.rem(r, ahead), lax.rem(r, 2)
-
-        @pl.when(r >= 2)
-        def _():
-            write(r - 2).wait()
-
-        for j in range(slots):
-            read_page(r, j).wait()
-            rows = pl.ds(j * page_len, page_len)
-            for part in range(2):
-                for i in range(pairs):
-                    both = jnp.concatenate([pages[slot, j, part, 2 * i], pages[slot, j, part, 2 * i + 1]], axis=-1)
-                    block[out_slot, part, i, rows, :] = both
-        write(r).start()
-
-        @pl.when(r + ahead < reqs)
-        def _():
-            for j in range(slots):
-                read_page(r + ahead, j).start()
-
-        return 0
-
-    lax.fori_loop(0, reqs, pack, 0)
     for r in (reqs - 2, reqs - 1):
         write(r).wait()
 
@@ -149,8 +155,8 @@
 
 
 def layer_kernel(layer, group, scale, q_ref, k_ref, v_ref, x_ref, gain_ref, kv_hbm, wo_hbm, wg_hbm, wu_hbm, wd_hbm, out_ref,
-                 kv, qbuf, obuf, loc, home, score, prob, rowwise, mid, peer_mid, normed, total, peer_total, wo, slab_in, slab_out,
-                 kv_sem, q_send, q_recv, o_send, o_recv, wo_sem, sems, peer_send, peer_recv):
+                 kv, qbuf, obuf, sbuf, loc, home, stat, share_w, score, prob, rowwise, mid, peer_mid, normed, total, peer_total, wo, slab_in, slab_out,
+                 kv_sem, q_send, q_recv, s_send, s_recv, o_send, o_recv, wo_sem, sems, peer_send, peer_recv):
     pairs, tokens, lanes = q_ref.shape
     half = pairs // 2
     rows = tokens // CHUNKS
@@ -182,6 +188,11 @@
     def o_copy(d, s, c):
         return pltpu.make_async_remote_copy(
             src_ref=obuf.at[d, s - 2, c], dst_ref=obuf.at[d, s - 1, c], send_sem=o_send.at[d, s - 2, c], recv_sem=o_recv.at[d, s - 1, c],
+            device_id={'pool': toward[d]}, device_id_type=pl.DeviceIdType.MESH)
+
+    def s_copy(d, s):
+        return pltpu.make_async_remote_copy(
+            src_ref=sbuf.at[d, s - 2], dst_ref=sbuf.at[d, s - 1], send_sem=s_send.at[d, s - 2], recv_sem=s_recv.at[d, s - 1],
             device_id={'pool': toward[d]}, device_id_type=pl.DeviceIdType.MESH)
 
     for d in range(2):
@@ -229,13 +240,13 @@
     row_low = row_lane < 64
     row_at = lax.broadcasted_iota(jnp.int32, (rows, lanes), 0)
 
-    def local_part(d, dest, query_at, key_at, val_at, causal):
+    def local_part(d, dest, which, query_at, key_at, val_at, causal):
         for j in range(half):
             score[d, j] = dot_t(query_at(j), block_diag(key_at(j), low_b, high_b)) * scale
+        tops = jnp.zeros((rows, lanes), F32)
+        sums = jnp.ones((rows, lanes), F32)
         for c in range(CHUNKS):
             here = slice(c * rows, (c + 1) * rows)
-            tops = jnp.zeros((rows, lanes), F32)
-            sums = jnp.ones((rows, lanes), F32)
             for j in range(half):
                 part = score[d, j, here]
                 if causal:
@@ -246,10 +257,10 @@
                 sum0 = jnp.sum(jnp.where(row_low, raised, 0.0), axis=1, keepdims=True)
                 sum1 = jnp.sum(jnp.where(row_low, 0.0, raised), axis=1, keepdims=True)
                 prob[d, j, here] = (raised * (1.0 / jnp.where(row_low, sum0, sum1))).astype(BF16)
-                at0, at1 = row_lane == j, row_lane == 64 + j
+                at0, at1 = row_lane == 16 * c + j, row_lane == 64 + 16 * c + j
                 tops = jnp.where(at0, top0, jnp.where(at1, top1, tops))
                 sums = jnp.where(at0, sum0, jnp.where(at1, sum1, sums))
-            dest[d, c, half] = tops + jnp.log(sums)
+        stat[which, d] = tops + jnp.log(sums)
         for j in range(half):
             out = jnp.dot(prob[d, j], block_diag(val_at(j), low_b, high_b), preferred_element_type=F32)
             for c in range(CHUNKS):
@@ -260,24 +271,25 @@
         joint = jnp.maximum(far, near) + jnp.log(1.0 + jnp.exp(-jnp.abs(gap)))
         return 1.0 / (1.0 + jnp.exp(-gap)), joint
 
-    def spread(stat, j):
-        return jnp.where(row_low, stat[:, j:j + 1], stat[:, 64 + j:65 + j])
-
     def merge(d, c, far, near):
-        weight, joint = weights(far[half], near[half])
-        outs = [near[j] + spread(weight, j) * (far[j] - near[j]) for j in range(half)]
-        return outs, joint
+        weight = share_w[d]
+        at = 16 * c
+        outs = []
+        for j in range(half):
+            spread = jnp.where(row_low, weight[:, at + j:at + j + 1], weight[:, 64 + at + j:65 + at + j])
+            outs.append(near[j] + spread * (far[j] - near[j]))
+        return outs
 
     for d in range(2):
         kv_copy(d, 0).wait()
         own = half * d
-        local_part(d, home, lambda j: q_ref[own + j], lambda j: kv[d, 0, 0, j], lambda j: kv[d, 0, 1, j], False)
-        local_part(d, loc, lambda j: q_ref[own + j], lambda j: k_ref[own + j], lambda j: v_ref[own + j], True)
+        local_part(d, home, 0, lambda j: q_ref[own + j], lambda j: kv[d, 0, 0, j], lambda j: kv[d, 0, 1, j], False)
+        local_part(d, loc, 1, lambda j: q_ref[own + j], lambda j: k_ref[own + j], lambda j: v_ref[own + j], True)
+        share_w[d], stat[0, d] = weights(stat[0, d], stat[1, d])
         for c in range(CHUNKS):
-            outs, joint = merge(d, c, home.at[d, c], loc.at[d, c])
+            outs = merge(d, c, home.at[d, c], loc.at[d, c])
             for j in range(half):
                 home[d, c, j] = outs[j]
-            home[d, c, half] = joint
 
     def step(s, _):
         for d in range(2):
@@ -289,7 +301,19 @@
 
         for d in range(2):
             kv_copy(d, s).wait()
-            local_part(d, loc, lambda j: qbuf[d, s, j], lambda j: kv[d, s, 0, j], lambda j: kv[d, s, 1, j], False)
+            local_part(d, loc, 1, lambda j: qbuf[d, s, j], lambda j: kv[d, s, 0, j], lambda j: kv[d, s, 1, j], False)
+
+        for d in range(2):
+            @pl.when(s == 1)
+            def _():
+                sbuf[d, 0] = stat[1, d]
+
+            @pl.when(s > 1)
+            def _():
+                s_copy(d, s).wait_recv()
+                share_w[d], sbuf[d, s - 1] = weights(sbuf[d, s - 1], stat[1, d])
+
+            s_copy(d, s + 1).start()
 
         @pl.when(s == 1)
         def _():
@@ -302,20 +326,22 @@
                 @pl.when(s > 1)
                 def _():
                     o_copy(d, s, c).wait_recv()
-                    outs, joint = merge(d, c, obuf.at[d, s - 1, c], loc.at[d, c])
+                    outs = merge(d, c, obuf.at[d, s - 1, c], loc.at[d, c])
                     for j in range(half):
                         obuf[d, s - 1, c, j] = outs[j]
-                    obuf[d, s - 1, c, half] = joint
 
                 o_copy(d, s + 1, c).start()
         return 0
 
     lax.fori_loop(1, group, step, 0)
 
+    for d in range(2):
+        s_copy(d, group).wait_recv()
+        share_w[d], _ = weights(sbuf[d, group - 1], stat[0, d])
     for c in range(CHUNKS):
         for d in range(2):
             o_copy(d, group, c).wait_recv()
-            outs, _ = merge(d, c, obuf.at[d, group - 1, c], home.at[d, c])
+            outs = merge(d, c, obuf.at[d, group - 1, c], home.at[d, c])
             for j in range(half):
                 at = (half * d + j) * lanes
                 rowwise[c * rows:(c + 1) * rows, at:at + lanes] = outs[j].astype(BF16)
@@ -327,10 +353,10 @@
         mid[:, cols] = (x_ref[:, cols].astype(F32) + proj).astype(BF16)
     share = to_peer(0, mid, peer_mid)
     share.start()
-    normed[:tokens] = rms_norm(mid[...], gain_ref[...])
+    normed[:tokens] = rms_norm(mid[...], gain_ref[layer:layer + 1])
     total[...] = jnp.zeros_like(total)
     share.wait_recv()
-    normed[tokens:] = rms_norm(peer_mid[...], gain_ref[...])
+    normed[tokens:] = rms_norm(peer_mid[...], gain_ref[layer:layer + 1])
 
     def one(n, _):
         slot = lax.rem(n, depth)
@@ -368,6 +394,7 @@
             def _():
                 q_copy(d, s).wait_send()
 
+            s_copy(d, s + 1).wait_send()
             for c in range(CHUNKS):
                 o_copy(d, s + 1, c).wait_send()
 
@@ -382,9 +409,12 @@
     scratch = [
         pltpu.VMEM((2, group, 2, half, tokens, lanes), BF16),
         pltpu.VMEM((2, group, half, tokens, lanes), BF16),
-        pltpu.VMEM((2, group, CHUNKS, half + 1, rows, lanes), F32),
-        pltpu.VMEM((2, CHUNKS, half + 1, rows, lanes), F32),
-        pltpu.VMEM((2, CHUNKS, half + 1, rows, lanes), F32),
+        pltpu.VMEM((2, group, CHUNKS, half, rows, lanes), F32),
+        pltpu.VMEM((2, group, rows, lanes), F32),
+        pltpu.VMEM((2, CHUNKS, half, rows, lanes), F32),
+        pltpu.VMEM((2, CHUNKS, half, rows, lanes), F32),
+        pltpu.VMEM((2, 2, rows, lanes), F32),
+        pltpu.VMEM((2, rows, lanes), F32),
         pltpu.VMEM((2, half, tokens, lanes), F32),
         pltpu.VMEM((2, half, tokens, lanes), BF16),
         pltpu.VMEM((tokens, attn), BF16),
@@ -396,6 +426,8 @@
         pltpu.VMEM((width // wo_tile, attn, wo_tile), BF16),
         pltpu.VMEM((depth, 2, width, tile), BF16),
         pltpu.VMEM((depth, tile, width), BF16),
+        sem((2, group)),
+        sem((2, group)),
         sem((2, group)),
         sem((2, group)),
         sem((2, group)),
@@ -429,8 +461,8 @@
         x = hid_local[0]
         for layer in range(layers):
             query, key, val, packed = layer_front(
-                x, idx, attn_norm[layer:layer + 1], cosine, sine, w_query, w_key, w_value, kv_heads, layer)
-            x = layer_rest(x, query, key, val, packed, mlp_norm[layer:layer + 1], w_out, w_gate, w_up, w_down, layer, group, dim ** -0.5)
+                x, idx, attn_norm, cosine, sine, w_query, w_key, w_value, kv_heads, layer)
+            x = layer_rest(x, query, key, val, packed, mlp_norm, w_out, w_gate, w_up, w_down, layer, group, dim ** -0.5)
         return x[None]
 
     data_specs = (P(None, ('rep', 'pool')), P(None, ('rep', 'pool'), None), P(('rep', 'pool')))

time: 284 us -> 262 us (0.923)
  Pallas kernels: 277 us -> 257 us
    pallas_call x2, Pallas kernels: 57.5 us -> 44.1 us  [layer_front(): pl.pallas_call(functools.partial(front_kernel, layer), in_specs=[pl.Block...]
    pallas_call x2, Pallas kernels: 219 us -> 213 us  [layer_rest(): pl.pallas_call(functools.partial(layer_kernel, layer, group, scale), out_...]
where the time goes in v2:
time: 262 us; the launch traced here: 261 us
  Pallas kernels  257 us (98%)
  local copies, waits for them, and re-layouts  3.05 us (1%)
    pallas_call x2, Pallas kernels, layer_rest(): pl.pallas_call(functools.partial(layer_kernel, layer, group, scale), out_...  213 us
    pallas_call x2, Pallas kernels, layer_front(): pl.pallas_call(functools.partial(front_kernel, layer), in_specs=[pl.Block...  44.1 us

profile of v2, /device:TPU:21, one launch (start us, length us, event | category | flops | bytes accessed | tf_op | source)
XLA Modules:
  0.0 261.3 jit_solution(13258693343880944049)
XLA Ops:
  0.0 1.4 copy.14.idx_ref
  1.4 0.2 fusion
  1.6 0.7 pad_maximum_fusion
  2.3 22.1 %layer_front.2 = (bf16[18,64,128]{2,1,0:T(8,128)(2,1)}, bf16[18,64,128]{2,1,0:T(8,128)(2,1)}, bf16[18,64,128]{2,1,0:T(8,128)(2,1)}, bf16[16,2,18,64,128]{4,3,2,1,0:T(8,128)(2,1)}) custom-call(s32[16,4]{1,0:T(8,128)} %copy.14.idx_ref, bf16[64,2304]{1,0:T(8,128)(2,1)} %bitcast.6, bf16[2,2304]{1,0:T(2,128)(2,1)} %gain_ref.6, ...), custom_call_target="tpu_custom_call" | custom-call | tf_op jit(solution)/shard_map/layer_front/pallas_call | solution.py:125
  24.4 109.2 %layer_rest.2.x_ref = bf16[64,2304]{1,0:T(8,128)(2,1)} custom-call(bf16[18,64,128]{2,1,0:T(8,128)(2,1)} %get-tuple-element.13.q_ref, bf16[18,64,128]{2,1,0:T(8,128)(2,1)} %get-tuple-element.14.k_ref, bf16[18,64,128]{2,1,0:T(8,128)(2,1)} %get-tuple-element.15.v_ref, bf16[64,2304]{1,0:T(8,128)(2,1)} %bitcast.7, bf16[2,2304]{1,0:T(2,128)(2,1)} %gain_ref.7, ...), custom_call_target="tpu_custom_call" | custom-call | tf_op jit(solution)/shard_map/layer_rest/pallas_call | solution.py:441
  133.6 22.0 %layer_front.3 = (bf16[18,64,128]{2,1,0:T(8,128)(2,1)}, bf16[18,64,128]{2,1,0:T(8,128)(2,1)}, bf16[18,64,128]{2,1,0:T(8,128)(2,1)}, bf16[16,2,18,64,128]{4,3,2,1,0:T(8,128)(2,1)}) custom-call(s32[16,4]{1,0:T(8,128)} %copy.14.idx_ref, bf16[64,2304]{1,0:T(8,128)(2,1)} %layer_rest.2.x_ref, bf16[2,2304]{1,0:T(2,128)(2,1)} %gain_ref.6, ...), custom_call_target="tpu_custom_call" | custom-call | tf_op jit(solution)/shard_map/layer_front/pallas_call | solution.py:125
  155.7 104.0 %layer_rest.3 = bf16[64,2304]{1,0:T(8,128)(2,1)} custom-call(bf16[18,64,128]{2,1,0:T(8,128)(2,1)} %get-tuple-element.17.q_ref, bf16[18,64,128]{2,1,0:T(8,128)(2,1)} %get-tuple-element.18.k_ref, bf16[18,64,128]{2,1,0:T(8,128)(2,1)} %get-tuple-element.19.v_ref, bf16[64,2304]{1,0:T(8,128)(2,1)} %layer_rest.2.x_ref, bf16[2,2304]{1,0:T(2,128)(2,1)} %gain_ref.7, ...), custom_call_target="tpu_custom_call" | custom-call | tf_op jit(solution)/shard_map/layer_rest/pallas_call | solution.py:441
  259.6 1.7 copy.16
  (2 shorter events, 0.0 us)

commit v3 on v2

--- a/solution.py
+++ b/solution.py
@@ -280,7 +280,7 @@
             outs.append(near[j] + spread * (far[j] - near[j]))
         return outs
 
-    for d in range(2):
+    def home_part(d):
         kv_copy(d, 0).wait()
         own = half * d
         local_part(d, home, 0, lambda j: q_ref[own + j], lambda j: kv[d, 0, 0, j], lambda j: kv[d, 0, 1, j], False)
@@ -331,6 +331,12 @@
                         obuf[d, s - 1, c, j] = outs[j]
 
                 o_copy(d, s + 1, c).start()
+
+        for d in range(2):
+            @pl.when(s == 4 + 3 * d)
+            def _():
+                home_part(d)
+
         return 0
 
     lax.fori_loop(1, group, step, 0)

time: 262 us -> 262 us (level)
  no operation moved by 1% of the time
where the time goes in v3:
time: 262 us; the launch traced here: 261 us
  Pallas kernels  257 us (98%)
  local copies, waits for them, and re-layouts  3.05 us (1%)
    pallas_call x2, Pallas kernels, layer_rest(): pl.pallas_call(functools.partial(layer_kernel, layer, group, scale), out_...  213 us
    pallas_call x2, Pallas kernels, layer_front(): pl.pallas_call(functools.partial(front_kernel, layer), in_specs=[pl.Block...  44.3 us

profile of v3, /device:TPU:21, one launch (start us, length us, event | category | flops | bytes accessed | tf_op | source)
XLA Modules:
  0.0 261.5 jit_solution(3969605502514282220)
XLA Ops:
  0.0 1.4 copy.14.idx_ref
  1.4 0.2 fusion
  1.6 0.7 pad_maximum_fusion
  2.3 22.1 %layer_front.2 = (bf16[18,64,128]{2,1,0:T(8,128)(2,1)}, bf16[18,64,128]{2,1,0:T(8,128)(2,1)}, bf16[18,64,128]{2,1,0:T(8,128)(2,1)}, bf16[16,2,18,64,128]{4,3,2,1,0:T(8,128)(2,1)}) custom-call(s32[16,4]{1,0:T(8,128)} %copy.14.idx_ref, bf16[64,2304]{1,0:T(8,128)(2,1)} %bitcast.6, bf16[2,2304]{1,0:T(2,128)(2,1)} %gain_ref.6, ...), custom_call_target="tpu_custom_call" | custom-call | tf_op jit(solution)/shard_map/layer_front/pallas_call | solution.py:125
  24.4 109.2 %layer_rest.2.x_ref = bf16[64,2304]{1,0:T(8,128)(2,1)} custom-call(bf16[18,64,128]{2,1,0:T(8,128)(2,1)} %get-tuple-element.13.q_ref, bf16[18,64,128]{2,1,0:T(8,128)(2,1)} %get-tuple-element.14.k_ref, bf16[18,64,128]{2,1,0:T(8,128)(2,1)} %get-tuple-element.15.v_ref, bf16[64,2304]{1,0:T(8,128)(2,1)} %bitcast.7, bf16[2,2304]{1,0:T(2,128)(2,1)} %gain_ref.7, ...), custom_call_target="tpu_custom_call" | custom-call | tf_op jit(solution)/shard_map/layer_rest/pallas_call | solution.py:447
  133.6 22.2 %layer_front.3 = (bf16[18,64,128]{2,1,0:T(8,128)(2,1)}, bf16[18,64,128]{2,1,0:T(8,128)(2,1)}, bf16[18,64,128]{2,1,0:T(8,128)(2,1)}, bf16[16,2,18,64,128]{4,3,2,1,0:T(8,128)(2,1)}) custom-call(s32[16,4]{1,0:T(8,128)} %copy.14.idx_ref, bf16[64,2304]{1,0:T(8,128)(2,1)} %layer_rest.2.x_ref, bf16[2,2304]{1,0:T(2,128)(2,1)} %gain_ref.6, ...), custom_call_target="tpu_custom_call" | custom-call | tf_op jit(solution)/shard_map/layer_front/pallas_call | solution.py:125
  155.8 104.0 %layer_rest.3 = bf16[64,2304]{1,0:T(8,128)(2,1)} custom-call(bf16[18,64,128]{2,1,0:T(8,128)(2,1)} %get-tuple-element.17.q_ref, bf16[18,64,128]{2,1,0:T(8,128)(2,1)} %get-tuple-element.18.k_ref, bf16[18,64,128]{2,1,0:T(8,128)(2,1)} %get-tuple-element.19.v_ref, bf16[64,2304]{1,0:T(8,128)(2,1)} %layer_rest.2.x_ref, bf16[2,2304]{1,0:T(2,128)(2,1)} %gain_ref.7, ...), custom_call_target="tpu_custom_call" | custom-call | tf_op jit(solution)/shard_map/layer_rest/pallas_call | solution.py:447
  259.8 1.7 copy.16
  (2 shorter events, 0.0 us)
